TPU v7x, 256 devices: a whole 4x4x8 slice. The times are simulated.
256 devices in a mesh: seq: 128 (over y_lo, z, x, core), head: 2 (over y_hi).
Axes of the slice: x: 4, y: 4 (y_hi: 2, y_lo: 2; y = y_hi * 2 + y_lo), z: 8, core: 2. Of those that a mesh axis runs over, the one named last changes fastest.
Arguments:
- query: bfloat16 [65536, 1024], P('seq', 'head'), may hold values from -6 to 6
- key_rows: bfloat16 [65536, 128], P('seq'), may hold values from -6 to 6
- value_rows: bfloat16 [65536, 128], P('seq'), may hold values from -6 to 6
- output: bfloat16 [65536, 1024], P('seq', 'head'), may hold values from -1.5 to 1.5
- grad_output: bfloat16 [65536, 1024], P('seq', 'head'), may hold values from -144 to 144
- log_norm: float32 [8, 65536], P('head', 'seq'), may hold values from 0.5 to 12
- stripe: int32 [128], replicated, may hold values from 0 to 127, each once
Outputs:
- grad_query: bfloat16 [65536, 1024], P('seq', 'head')
- grad_key: bfloat16 [65536, 128], P(('seq', 'head'))
- grad_value: bfloat16 [65536, 128], P(('seq', 'head'))
Inputs may be any that keep to these rules, and one draw needn't show every extreme that they name: stripe is a permutation of 0 to 127.
All inputs are finite; a program needn't handle non-finite values.
Results may differ from a plain program's by a relative error of at most 0.0051.
Values may be sent and summed in bfloat16 or wider, within the bound.
A program may use at most 192 MiB of HBM per device.

v0:
```python
import functools
import math

import jax
import jax.numpy as jnp
from jax import lax
from jax.experimental import pallas as pl
from jax.experimental.pallas import tpu as pltpu
from jax.sharding import PartitionSpec as P

F32 = jnp.float32
BF16 = jnp.bfloat16
ROWS = 512
DH = 128
HEADS = 4
TILE = 128
TILES = ROWS // TILE
PAIR = 2 * TILE
UNITS = HEADS * ROWS // PAIR
HALF = ROWS // 2
LOG2E = math.log2(math.e)
SCALE = 1.0 / math.sqrt(DH)

OWN, E, PE, L, PL, PF, F, C = range(8)


def dot(a, b):
    return lax.dot_general(a, b, (((1,), (0,)), ((), ())), preferred_element_type=F32)


def lay_out(q_ref, o_ref, g_ref, lse_ref, q2, g2, qt, gt, lse2, delta):
    for h in range(HEADS):
        hp, e = divmod(h, 2)
        cols = slice(h * DH, (h + 1) * DH)
        q_h = q_ref[:, cols]
        g_h = g_ref[:, cols]
        q_t = q_h.T
        g_t = g_h.T
        sums = jnp.sum(g_t.astype(F32) * o_ref[:, cols].T.astype(F32), axis=0, keepdims=True)
        for j in range(TILES):
            u = hp * TILES + j
            at = u * PAIR + e * TILE
            rows = slice(j * TILE, (j + 1) * TILE)
            q2[at : at + TILE, :] = q_h[rows]
            g2[at : at + TILE, :] = g_h[rows]
            qt[:, at : at + TILE] = q_t[:, rows]
            gt[:, at : at + TILE] = g_t[:, rows]
            lse2[u : u + 1, e * TILE : (e + 1) * TILE] = lse_ref[h : h + 1, rows] * LOG2E
            delta[u : u + 1, e * TILE : (e + 1) * TILE] = sums[:, rows]


def pair_terms(k, v, qt, gt, lse2, delta, u, j, open_diag):
    depth = TILE * (j + 1)
    cols = slice(u * PAIR, (u + 1) * PAIR)
    scores = dot(k[0:depth, :], qt[:, cols])
    grad_p = dot(v[0:depth, :], gt[:, cols])
    p = jnp.exp2(scores * (LOG2E * SCALE) - lse2[u : u + 1, :])
    key_row = lax.broadcasted_iota(jnp.int32, (TILE, PAIR), 0)
    query_row = lax.broadcasted_iota(jnp.int32, (TILE, PAIR), 1) % TILE
    last = jnp.where(key_row < query_row + open_diag, p[depth - TILE :], 0.0)
    p = last if j == 0 else jnp.concatenate([p[: depth - TILE], last], 0)
    grad_s = ((p * SCALE) * (grad_p - delta[u : u + 1, :])).astype(BF16)
    return p.astype(BF16), grad_s


def block(kv, acc, open_diag, kt, q2, g2, qt, gt, lse2, delta, dqt):
    k, v = kv.at[0], kv.at[1]
    kt[...] = k[...].T
    for j in reversed(range(TILES)):
        depth = TILE * (j + 1)
        p0, s0 = pair_terms(k, v, qt, gt, lse2, delta, j, j, open_diag)
        p1, s1 = pair_terms(k, v, qt, gt, lse2, delta, TILES + j, j, open_diag)
        c0 = slice(j * PAIR, (j + 1) * PAIR)
        c1 = slice((TILES + j) * PAIR, (TILES + j + 1) * PAIR)
        grad_v = dot(p0, g2[c0, :]) + dot(p1, g2[c1, :])
        grad_k = dot(s0, q2[c0, :]) + dot(s1, q2[c1, :])
        if j == TILES - 1:
            acc[1, 0:depth, :] = grad_v
            acc[0, 0:depth, :] = grad_k
        else:
            acc[1, 0:depth, :] += grad_v
            acc[0, 0:depth, :] += grad_k
        dqt[:, c0] += dot(kt[:, 0:depth], s0)
        dqt[:, c1] += dot(kt[:, 0:depth], s1)


def kernel(
    n,
    stripe,
    q_hbm,
    k_hbm,
    v_hbm,
    o_hbm,
    g_hbm,
    lse_hbm,
    dq_hbm,
    dk_ref,
    dv_ref,
    q_ref,
    o_ref,
    g_ref,
    lse_ref,
    q2,
    g2,
    qt,
    gt,
    lse2,
    delta,
    kt,
    dqt,
    dq_ref,
    kvs,
    accs,
    p_out,
    p_in,
    y_out,
    y_in,
    x_out,
    d_out,
    r_in,
    load_sem,
    kv_send,
    kv_recv,
    p_send,
    p_recv,
    y_send,
    y_recv,
    x_send,
    d_send,
    r_recv,
    out_sem,
):
    me = lax.axis_index("seq")
    head = lax.axis_index("head")
    core = lax.rem(me, 2)

    def at(offset):
        return {"seq": lax.rem(me + offset + n, n), "head": head}

    partner = at(1 - 2 * core)
    across = {"seq": me, "head": 1 - head}

    loads = [
        pltpu.make_async_copy(k_hbm, kvs.at[OWN, 0], load_sem.at[0]),
        pltpu.make_async_copy(v_hbm, kvs.at[OWN, 1], load_sem.at[1]),
        pltpu.make_async_copy(q_hbm, q_ref, load_sem.at[2]),
        pltpu.make_async_copy(g_hbm, g_ref, load_sem.at[3]),
        pltpu.make_async_copy(o_hbm, o_ref, load_sem.at[4]),
        pltpu.make_async_copy(lse_hbm, lse_ref, load_sem.at[5]),
    ]
    for load in loads:
        load.start()

    barrier = pltpu.get_barrier_semaphore()
    peers = [partner, across, at(2), at(-2), at(6), at(-6), at(4), at(-4), at(14 * core - 7)]
    for peer in peers:
        pl.semaphore_signal(barrier, inc=1, device_id=peer, device_id_type=pl.DeviceIdType.MESH)

    def remote(src, dst, send, recv, to):
        return pltpu.make_async_remote_copy(
            src_ref=src, dst_ref=dst, send_sem=send, recv_sem=recv, device_id=to, device_id_type=pl.DeviceIdType.MESH
        )

    def pass_kv(src, dst, to):
        return remote(kvs.at[src], kvs.at[dst], kv_send.at[dst], kv_recv.at[dst], to)

    send_e = pass_kv(OWN, E, at(2 + 4 * core))
    send_l = pass_kv(OWN, L, at(6 - 4 * core))
    send_c = pass_kv(OWN, C, at(1 + 6 * core))
    pass_e = pass_kv(E, PE, partner)
    pass_on = pass_kv(E, F, at(2 - 4 * core))
    pass_l = pass_kv(L, PL, partner)
    pass_f = pass_kv(F, PF, partner)
    to_partner = [remote(p_out.at[m], p_in.at[m], p_send.at[m], p_recv.at[m], partner) for m in range(3)]
    exchange = [remote(y_out.at[m], y_in.at[m], y_send.at[m], y_recv.at[m], across) for m in range(3)]
    owners = [at(-2 - 4 * core), at(-6 + 4 * core), at(-4), at(-7 + 6 * core)]
    to_owner = [remote(x_out.at[m], r_in.at[m], x_send.at[m], r_recv.at[m], owners[m]) for m in range(2)]

    def both(m, o, into):
        far = {"seq": owners[o]["seq"], "head": 1 - head}
        return [
            remote(d_out.at[m], r_in.at[into], d_send.at[m], r_recv.at[into], owners[o]),
            remote(d_out.at[m + 1], r_in.at[into + 1], d_send.at[m + 1], r_recv.at[into + 1], far),
        ]

    direct = both(0, 2, 2) + both(2, 3, 4)

    mine = pl.ds(pl.multiple_of(head * HALF, HALF), HALF)
    other = pl.ds(pl.multiple_of((1 - head) * HALF, HALF), HALF)

    loads[0].wait()
    loads[1].wait()
    pl.semaphore_wait(barrier, len(peers))
    send_e.start()
    send_c.start()
    for load in loads[2:]:
        load.wait()
    lay_out(q_ref, o_ref, g_ref, lse_ref, q2, g2, qt, gt, lse2, delta)
    dqt[...] = jnp.zeros_like(dqt)
    own_stripe = stripe[me]
    back = [(0, 0), (2, 4), (5, -2), (6, -4), (1, 6), (3, 2), (4, 0), (7, -6)]

    def step(s, carry):
        behind = jnp.int32(0)
        for m in range(1, 8):
            behind = jnp.where(s == m, back[m][0] + back[m][1] * core, behind)

        @pl.when((s != OWN) & (s != F))
        def _():
            pltpu.make_async_copy(kvs.at[s], kvs.at[s], kv_recv.at[s]).wait()

        @pl.when(s == E)
        def _():
            pass_on.start()
            pass_e.start()

        @pl.when(s == L)
        def _():
            pass_l.start()

        @pl.when(s == PL)
        def _():
            pass_on.wait_recv()
            pass_f.start()

        source = lax.rem(me - behind + n, n)
        open_diag = jnp.where(stripe[source] <= own_stripe, 1, 0)
        block(kvs.at[s], accs.at[s], open_diag, kt, q2, g2, qt, gt, lse2, delta, dqt)

        @pl.when(s == OWN)
        def _():
            y_out[2] = accs[OWN, :, other, :].astype(BF16)
            exchange[2].start()
            send_e.wait_send()
            send_l.start()

        for m, (part, when) in enumerate(((PE, PE), (PL, PL), (PF, PF))):

            @pl.when(s == when)
            def _():
                p_out[m] = accs[part].astype(BF16)
                to_partner[m].start()

        for m, (part, when) in enumerate(((E, L), (L, PF))):

            @pl.when(s == when)
            def _():
                to_partner[m].wait_recv()
                y_out[m] = (accs[part, :, other, :] + p_in[m, :, other, :].astype(F32)).astype(BF16)
                exchange[m].start()

        def finish(m, part):
            exchange[m].wait_recv()
            total = accs[part, :, mine, :] + p_in[m, :, mine, :].astype(F32) + y_in[m].astype(F32)
            x_out[m] = total.astype(BF16)
            to_owner[m].start()

        @pl.when(s == F)
        def _():
            to_partner[2].wait_recv()
            d_out[1] = (accs[F, :, other, :] + p_in[2, :, other, :].astype(F32)).astype(BF16)
            direct[1].start()
            d_out[0] = (accs[F, :, mine, :] + p_in[2, :, mine, :].astype(F32)).astype(BF16)
            direct[0].start()
            finish(0, E)

        @pl.when(s == C)
        def _():
            d_out[3] = accs[C, :, other, :].astype(BF16)
            direct[3].start()
            d_out[2] = accs[C, :, mine, :].astype(BF16)
            direct[2].start()
            finish(1, L)

        return carry

    lax.fori_loop(0, 8, step, 0)

    for h in range(HEADS):
        hp, e = divmod(h, 2)
        for j in range(TILES):
            begin = (hp * TILES + j) * PAIR + e * TILE
            tile = dqt[:, begin : begin + TILE].astype(BF16).T
            dq_ref[j * TILE : (j + 1) * TILE, h * DH : (h + 1) * DH] = tile
    write = pltpu.make_async_copy(dq_ref, dq_hbm, out_sem)
    write.start()

    total = accs[OWN, :, mine, :]
    exchange[2].wait_recv()
    total = total + y_in[2].astype(F32)
    for copy in to_owner:
        copy.wait_recv()
    for copy in direct:
        copy.wait_recv()
    for m in range(6):
        total = total + r_in[m].astype(F32)
    dk_ref[...] = total[0].astype(BF16)
    dv_ref[...] = total[1].astype(BF16)
    for copy in [send_l, send_c, pass_e, pass_on, pass_l, pass_f] + to_partner + exchange + to_owner + direct:
        copy.wait_send()
    write.wait()


def solution(mesh):
    n = mesh.shape["seq"]
    half = (2, HALF, DH)

    def shards(query, key_rows, value_rows, output, grad_output, log_norm, stripe):
        anywhere = pl.BlockSpec(memory_space=pl.ANY)
        vmem = pl.BlockSpec(memory_space=pltpu.VMEM)
        dma = pltpu.SemaphoreType.DMA
        return pl.pallas_call(
            functools.partial(kernel, n),
            out_shape=(
                jax.ShapeDtypeStruct(query.shape, BF16),
                jax.ShapeDtypeStruct((HALF, DH), BF16),
                jax.ShapeDtypeStruct((HALF, DH), BF16),
            ),
            in_specs=[pl.BlockSpec(memory_space=pltpu.SMEM)] + [anywhere] * 6,
            out_specs=(anywhere, vmem, vmem),
            scratch_shapes=[
                pltpu.VMEM((ROWS, HEADS * DH), BF16),
                pltpu.VMEM((ROWS, HEADS * DH), BF16),
                pltpu.VMEM((ROWS, HEADS * DH), BF16),
                pltpu.VMEM((HEADS, ROWS), F32),
                pltpu.VMEM((UNITS * PAIR, DH), BF16),
                pltpu.VMEM((UNITS * PAIR, DH), BF16),
                pltpu.VMEM((DH, UNITS * PAIR), BF16),
                pltpu.VMEM((DH, UNITS * PAIR), BF16),
                pltpu.VMEM((UNITS, PAIR), F32),
                pltpu.VMEM((UNITS, PAIR), F32),
                pltpu.VMEM((DH, ROWS), BF16),
                pltpu.VMEM((DH, UNITS * PAIR), F32),
                pltpu.VMEM((ROWS, HEADS * DH), BF16),
                pltpu.VMEM((8, 2, ROWS, DH), BF16),
                pltpu.VMEM((8, 2, ROWS, DH), F32),
                pltpu.VMEM((3, 2, ROWS, DH), BF16),
                pltpu.VMEM((3, 2, ROWS, DH), BF16),
                pltpu.VMEM((3,) + half, BF16),
                pltpu.VMEM((3,) + half, BF16),
                pltpu.VMEM((2,) + half, BF16),
                pltpu.VMEM((4,) + half, BF16),
                pltpu.VMEM((6,) + half, BF16),
                dma((6,)),
                dma((8,)),
                dma((8,)),
                dma((3,)),
                dma((3,)),
                dma((3,)),
                dma((3,)),
                dma((2,)),
                dma((4,)),
                dma((6,)),
                dma,
            ],
            compiler_params=pltpu.CompilerParams(
                collective_id=0, has_side_effects=True, vmem_limit_bytes=60 * 2**20
            ),
            name="window_grads",
        )(stripe, query, key_rows, value_rows, output, grad_output, log_norm)

    placed = (
        P("seq", "head"),
        P("seq", None),
        P("seq", None),
        P("seq", "head"),
        P("seq", "head"),
        P("head", "seq"),
        P(),
    )
    return jax.shard_map(
        shards,
        mesh=mesh,
        in_specs=placed,
        out_specs=(P("seq", "head"), P(("seq", "head"), None), P(("seq", "head"), None)),
        check_vma=False,
    )
```

profile of v0, /device:TPU:8, one launch (start us, length us, event | category | flops | bytes accessed | tf_op | source)
XLA Modules:
  0.0 56.4 jit_solution(16946198497897390962)
XLA Ops:
  0.6 52.3 %window_grads.1 = (bf16[512,512]{1,0:T(8,128)(2,1)}, bf16[256,128]{1,0:T(8,128)(2,1)}, bf16[256,128]{1,0:T(8,128)(2,1)}) custom-call(s32[128]{0:T(128)} %stripe.1, bf16[512,512]{1,0:T(8,128)(2,1)} %q_hbm.1, bf16[512,128]{1,0:T(8,128)(2,1)} %k_hbm.1, bf16[512,128]{1,0:T(8,128)(2,1)} %v_hbm.1, bf16[512,512]{1,0:T(8,128)(2,1)} %o_hbm.1, ...), custom_call_target="tpu_custom_call" | custom-call | tf_op jit(solution)/shard_map/window_grads/pallas_call | solution.py:312
  53.0 0.0 copy-start.1
  53.0 1.9 %copy.13 = bf16[512,512]{1,0:T(8,128)(2,1)} copy(bf16[512,512]{1,0:T(8,128)(2,1)} %get-tuple-element.6) | data formatting | bytes 1048576
  54.9 0.0 copy-done.1
  54.9 0.0 copy-start
  54.9 0.6 %copy.14 = bf16[256,128]{1,0:T(8,128)(2,1)} copy(bf16[256,128]{1,0:T(8,128)(2,1)S(1)} %copy-done.1) | data formatting | bytes 131072
  55.5 0.2 copy-done
  55.7 0.6 %copy.15 = bf16[256,128]{1,0:T(8,128)(2,1)} copy(bf16[256,128]{1,0:T(8,128)(2,1)S(1)} %copy-done) | data formatting | bytes 131072
Async XLA Ops:
  53.0 1.9 %copy-start.1 = (bf16[256,128]{1,0:T(8,128)(2,1)S(1)}, bf16[256,128]{1,0:T(8,128)(2,1)}, u32[]{:S(2)}) copy-start(bf16[256,128]{1,0:T(8,128)(2,1)} %get-tuple-element.7) | copy-start | bytes 196612
  54.9 0.9 %copy-start = (bf16[256,128]{1,0:T(8,128)(2,1)S(1)}, bf16[256,128]{1,0:T(8,128)(2,1)}, u32[]{:S(2)}) copy-start(bf16[256,128]{1,0:T(8,128)(2,1)} %get-tuple-element.8) | copy-start | bytes 196612
where the time goes:
time: 56.5 us; the launch traced here: 56.4 us
  Pallas kernels  52.3 us (93%)
  local copies, waits for them, and re-layouts  3.4 us (6%)
  between operations  0.65 us (1%)
    pallas_call x1, Pallas kernels, shards(): pl.pallas_call(functools.partial(kernel, n), out_shape=(jax.ShapeDtypeStr...  52.3 us
    unnamed x7, local copies, waits for them, and re-layouts  3.4 us

commit v1 on v0

v1 whole, which is shorter than its diff:
```python
import functools
import math

import jax
import jax.numpy as jnp
from jax import lax
from jax.experimental import pallas as pl
from jax.experimental.pallas import tpu as pltpu
from jax.sharding import PartitionSpec as P

F32 = jnp.float32
BF16 = jnp.bfloat16
ROWS = 512
DH = 128
HEADS = 4
TILE = 128
TILES = ROWS // TILE
WIDE = HEADS * TILE
HALF = ROWS // 2
LOG2E = math.log2(math.e)
SCALE = 1.0 / math.sqrt(DH)

OWN, E, PE, C, PF, F, PL, L = range(8)


def dot(a, b):
    return lax.dot_general(a, b, (((1,), (0,)), ((), ())), preferred_element_type=F32)


def lay_out(q_ref, o_ref, g_ref, lse_ref, q2, g2, qt, gt, lse2, delta):
    for h in range(HEADS):
        cols = slice(h * DH, (h + 1) * DH)
        q_h = q_ref[:, cols]
        g_h = g_ref[:, cols]
        q_t = q_h.T
        g_t = g_h.T
        sums = jnp.sum(g_t.astype(F32) * o_ref[:, cols].T.astype(F32), axis=0, keepdims=True)
        for j in range(TILES):
            at = j * WIDE + h * TILE
            rows = slice(j * TILE, (j + 1) * TILE)
            q2[at : at + TILE, :] = q_h[rows]
            g2[at : at + TILE, :] = g_h[rows]
            qt[:, at : at + TILE] = q_t[:, rows]
            gt[:, at : at + TILE] = g_t[:, rows]
            lse2[j : j + 1, h * TILE : (h + 1) * TILE] = lse_ref[h : h + 1, rows] * LOG2E
            delta[j : j + 1, h * TILE : (h + 1) * TILE] = sums[:, rows]


def half_block(part, kv, acc, open_diag, kt, q2, g2, qt, gt, lse2, delta, dqt):
    k, v = kv.at[0], kv.at[1]
    kt[...] = k[...].T
    first = True
    for j in reversed(range(2 * part, TILES)):
        rows = min(HALF, TILE * (j + 1) - HALF * part)
        cols = slice(j * WIDE, (j + 1) * WIDE)
        scores = dot(k[0:rows, :], qt[:, cols])
        grad_p = dot(v[0:rows, :], gt[:, cols])
        p = jnp.exp2(scores * (LOG2E * SCALE) - lse2[j : j + 1, :])
        if HALF * part + rows == TILE * (j + 1):
            key_row = lax.broadcasted_iota(jnp.int32, (TILE, WIDE), 0)
            query_row = lax.broadcasted_iota(jnp.int32, (TILE, WIDE), 1) % TILE
            last = jnp.where(key_row < query_row + open_diag, p[rows - TILE :], 0.0)
            p = last if rows == TILE else jnp.concatenate([p[: rows - TILE], last], 0)
        grad_s = ((p * SCALE) * (grad_p - delta[j : j + 1, :])).astype(BF16)
        grad_v = dot(p.astype(BF16), g2[cols, :])
        grad_k = dot(grad_s, q2[cols, :])
        if first:
            acc[1, 0:rows, :] = grad_v
            acc[0, 0:rows, :] = grad_k
        else:
            acc[1, 0:rows, :] += grad_v
            acc[0, 0:rows, :] += grad_k
        first = False
        dqt[:, cols] += dot(kt[:, 0:rows], grad_s)


def kernel(
    n,
    stripe,
    q_hbm,
    k_hbm,
    v_hbm,
    o_hbm,
    g_hbm,
    lse_hbm,
    dq_ref,
    dk_ref,
    dv_ref,
    q_ref,
    o_ref,
    g_ref,
    lse_ref,
    q2,
    g2,
    qt,
    gt,
    lse2,
    delta,
    kt,
    dqt,
    kvs,
    accs,
    p_out,
    p_in,
    r_out,
    own_out,
    r_in,
    load_sem,
    kv_send,
    kv_recv,
    p_send,
    p_recv,
    r_send,
    own_send,
    r_recv,
):
    me = lax.axis_index("seq")
    head = lax.axis_index("head")
    core = lax.rem(me, 2)

    def seq(offset):
        return lax.rem(me + offset + n, n)

    def at(offset):
        return {"seq": seq(offset), "head": head}

    partner = at(1 - 2 * core)
    across = {"seq": me, "head": 1 - head}

    loads = []
    for source, into in ((k_hbm, 0), (v_hbm, 1)):
        for part in range(2):
            rows = source.at[pl.ds(part * HALF, HALF)]
            loads.append(pltpu.make_async_copy(rows, kvs.at[OWN, part, into], load_sem.at[len(loads)]))
    for source, into in ((q_hbm, q_ref), (g_hbm, g_ref), (o_hbm, o_ref), (lse_hbm, lse_ref)):
        loads.append(pltpu.make_async_copy(source, into, load_sem.at[len(loads)]))
    for load in loads:
        load.start()

    barrier = pltpu.get_barrier_semaphore()
    peers = [partner, across, at(2), at(-2), at(6), at(-6), at(4), at(-4), at(14 * core - 7)]
    peers += [{"seq": peer["seq"], "head": 1 - head} for peer in [partner] + peers[2:]]
    for peer in peers:
        pl.semaphore_signal(barrier, inc=1, device_id=peer, device_id_type=pl.DeviceIdType.MESH)

    def remote(src, dst, send, recv, to):
        return pltpu.make_async_remote_copy(
            src_ref=src, dst_ref=dst, send_sem=send, recv_sem=recv, device_id=to, device_id_type=pl.DeviceIdType.MESH
        )

    def pass_kv(src, dst, to):
        return [
            remote(kvs.at[src, part], kvs.at[dst, part], kv_send.at[dst, part], kv_recv.at[dst, part], to)
            for part in range(2)
        ]

    send_e = pass_kv(OWN, E, at(2 + 4 * core))
    send_l = pass_kv(OWN, L, at(6 - 4 * core))
    send_c = pass_kv(OWN, C, at(1 + 6 * core))
    pass_e = pass_kv(E, PE, partner)
    pass_on = pass_kv(E, F, at(2 - 4 * core))
    pass_l = pass_kv(L, PL, partner)
    pass_f = pass_kv(F, PF, partner)
    to_partner = [
        [remote(p_out.at[m, part], p_in.at[m, part], p_send.at[m, part], p_recv.at[m, part], partner) for part in range(2)]
        for m in range(3)
    ]
    owners = [-2 - 4 * core, -6 + 4 * core, -4, -7 + 6 * core]

    def to_owner(m, part):
        slot = 2 * m + jnp.where(head == part, 0, 1)
        to = {"seq": seq(owners[m]), "head": part}
        return remote(r_out.at[m, part], r_in.at[slot], r_send.at[m, part], r_recv.at[slot], to)

    returns = [[to_owner(m, part) for part in range(2)] for m in range(4)]
    own_half = remote(own_out, r_in.at[8], own_send, r_recv.at[8], across)

    for load in loads[:4]:
        load.wait()
    pl.semaphore_wait(barrier, len(peers))
    for copy in send_e:
        copy.start()
    for load in loads[4:]:
        load.wait()
    lay_out(q_ref, o_ref, g_ref, lse_ref, q2, g2, qt, gt, lse2, delta)
    dqt[...] = jnp.zeros_like(dqt)
    own_stripe = stripe[me]
    back = {OWN: (0, 0), E: (2, 4), PE: (5, -2), C: (7, -6), PF: (3, 2), F: (4, 0), PL: (1, 6), L: (6, -4)}

    def relay(part):
        return [(E, send_e[part], [pass_on[part], pass_e[part]]), (C, pass_on[part], [pass_f[part]]), (F, send_l[part], [pass_l[part]])]

    def begin(s, part):
        @pl.when((s == PE) | (s == C) | (s == PF) | (s == PL))
        def _():
            pltpu.make_async_copy(kvs.at[s, part], kvs.at[s, part], kv_recv.at[s, part]).wait()

        for when, came, copies in relay(part):

            @pl.when(s == when)
            def _():
                came.wait_recv()
                for copy in copies:
                    copy.start()

    def send_back(m, block, part):
        total = accs[block, part]
        if m < 3:
            to_partner[m][part].wait_recv()
            total = total + p_in[m, part].astype(F32)
        r_out[m, part] = total.astype(BF16)
        returns[m][part].start()

    def finish(s, part):
        @pl.when((s == OWN) & (head != part))
        def _():
            own_out[...] = accs[OWN, part].astype(BF16)
            own_half.start()

        if part == 1:

            @pl.when(s == OWN)
            def _():
                for copy in send_c:
                    copy.start()

            @pl.when(s == E)
            def _():
                for copy in send_l:
                    copy.start()

        for m, block in enumerate((PE, PL, PF)):

            @pl.when(s == block)
            def _():
                p_out[m, part] = accs[block, part].astype(BF16)
                to_partner[m][part].start()

        @pl.when(s == C)
        def _():
            if part == 0:
                send_back(0, E, 0)
                send_back(0, E, 1)
            send_back(3, C, part)

        for m, block in ((2, F), (1, L)):

            @pl.when(s == block)
            def _():
                send_back(m, block, part)

    def step(s, carry):
        behind = jnp.int32(0)
        for block, (far, more) in back.items():
            behind = jnp.where(s == block, far + more * core, behind)
        open_diag = jnp.where(stripe[seq(-behind)] <= own_stripe, 1, 0)
        for part in range(2):
            begin(s, part)
            half_block(part, kvs.at[s, part], accs.at[s, part], open_diag, kt, q2, g2, qt, gt, lse2, delta, dqt)
            finish(s, part)
        return carry

    lax.fori_loop(0, 8, step, 0)

    for h in range(HEADS):
        for j in range(TILES):
            begin_col = j * WIDE + h * TILE
            tile = dqt[:, begin_col : begin_col + TILE].astype(BF16).T
            dq_ref[j * TILE : (j + 1) * TILE, h * DH : (h + 1) * DH] = tile

    total = accs[OWN, head]
    for slot in (6, 7, 8, 0, 1, 4, 5, 2, 3):
        pltpu.make_async_copy(r_in.at[slot], r_in.at[slot], r_recv.at[slot]).wait()
        total = total + r_in[slot].astype(F32)
    dk_ref[...] = total[0].astype(BF16)
    dv_ref[...] = total[1].astype(BF16)
    for copies in [send_e, send_l, send_c, pass_e, pass_on, pass_l, pass_f] + to_partner + returns + [[own_half]]:
        for copy in copies:
            copy.wait_send()


def solution(mesh):
    n = mesh.shape["seq"]
    half = (2, HALF, DH)

    def shards(query, key_rows, value_rows, output, grad_output, log_norm, stripe):
        anywhere = pl.BlockSpec(memory_space=pl.ANY)
        vmem = pl.BlockSpec(memory_space=pltpu.VMEM)
        dma = pltpu.SemaphoreType.DMA
        return pl.pallas_call(
            functools.partial(kernel, n),
            out_shape=(
                pltpu.VMEM(query.shape, BF16),
                pltpu.VMEM((HALF, DH), BF16),
                pltpu.VMEM((HALF, DH), BF16),
            ),
            in_specs=[pl.BlockSpec(memory_space=pltpu.SMEM)] + [anywhere] * 6,
            out_specs=(vmem, vmem, vmem),
            scratch_shapes=[
                pltpu.VMEM((ROWS, HEADS * DH), BF16),
                pltpu.VMEM((ROWS, HEADS * DH), BF16),
                pltpu.VMEM((ROWS, HEADS * DH), BF16),
                pltpu.VMEM((HEADS, ROWS), F32),
                pltpu.VMEM((TILES * WIDE, DH), BF16),
                pltpu.VMEM((TILES * WIDE, DH), BF16),
                pltpu.VMEM((DH, TILES * WIDE), BF16),
                pltpu.VMEM((DH, TILES * WIDE), BF16),
                pltpu.VMEM((TILES, WIDE), F32),
                pltpu.VMEM((TILES, WIDE), F32),
                pltpu.VMEM((DH, HALF), BF16),
                pltpu.VMEM((DH, TILES * WIDE), F32),
                pltpu.VMEM((8, 2) + half, BF16),
                pltpu.VMEM((8, 2) + half, F32),
                pltpu.VMEM((3, 2) + half, BF16),
                pltpu.VMEM((3, 2) + half, BF16),
                pltpu.VMEM((4, 2) + half, BF16),
                pltpu.VMEM(half, BF16),
                pltpu.VMEM((9,) + half, BF16),
                dma((8,)),
                dma((8, 2)),
                dma((8, 2)),
                dma((3, 2)),
                dma((3, 2)),
                dma((4, 2)),
                dma,
                dma((9,)),
            ],
            compiler_params=pltpu.CompilerParams(
                collective_id=0, has_side_effects=True, vmem_limit_bytes=60 * 2**20
            ),
            name="window_grads",
        )(stripe, query, key_rows, value_rows, output, grad_output, log_norm)

    placed = (
        P("seq", "head"),
        P("seq", None),
        P("seq", None),
        P("seq", "head"),
        P("seq", "head"),
        P("head", "seq"),
        P(),
    )
    return jax.shard_map(
        shards,
        mesh=mesh,
        in_specs=placed,
        out_specs=(P("seq", "head"), P(("seq", "head"), None), P(("seq", "head"), None)),
        check_vma=False,
    )
```

time: 56.5 us -> 48.9 us (0.87)
  Pallas kernels: 52.3 us -> 46.1 us
  local copies, waits for them, and re-layouts: 3.4 us -> 2.05 us
    pallas_call x1, Pallas kernels: 52.3 us -> 46.1 us  [shards(): pl.pallas_call(functools.partial(kernel, n), out_shape=(pltpu.VMEM(query....]
    unnamed x7 -> x3, local copies, waits for them, and re-layouts: 3.4 us -> 2.05 us
where the time goes in v1:
time: 48.9 us; the launch traced here: 48.8 us
  Pallas kernels  46.1 us (94%)
  local copies, waits for them, and re-layouts  2.05 us (4%)
  between operations  0.64 us (1%)
    pallas_call x1, Pallas kernels, shards(): pl.pallas_call(functools.partial(kernel, n), out_shape=(pltpu.VMEM(query....  46.1 us
    unnamed x3, local copies, waits for them, and re-layouts  2.05 us

profile of v1, /device:TPU:8, one launch (start us, length us, event | category | flops | bytes accessed | tf_op | source)
XLA Modules:
  0.0 48.8 jit_solution(13120481388684487919)
XLA Ops:
  0.6 46.1 %window_grads.1 = (bf16[512,512]{1,0:T(8,128)(2,1)S(1)}, bf16[256,128]{1,0:T(8,128)(2,1)S(1)}, bf16[256,128]{1,0:T(8,128)(2,1)S(1)}) custom-call(s32[128]{0:T(128)} %stripe.1, bf16[512,512]{1,0:T(8,128)(2,1)} %q_hbm.1, bf16[512,128]{1,0:T(8,128)(2,1)} %k_hbm.1, bf16[512,128]{1,0:T(8,128)(2,1)} %v_hbm.1, bf16[512,512]{1,0:T(8,128)(2,1)} %o_hbm.1, ...), custom_call_target="tpu_custom_call" | custom-call | tf_op jit(solution)/shard_map/window_grads/pallas_call | solution.py:290
  46.7 0.8 %copy.13 = bf16[512,512]{1,0:T(8,128)(2,1)} copy(bf16[512,512]{1,0:T(8,128)(2,1)S(1)} %get-tuple-element.3) | data formatting | bytes 1048576
  47.5 0.6 %copy.14 = bf16[256,128]{1,0:T(8,128)(2,1)} copy(bf16[256,128]{1,0:T(8,128)(2,1)S(1)} %get-tuple-element.4) | data formatting | bytes 131072
  48.2 0.6 %copy.15 = bf16[256,128]{1,0:T(8,128)(2,1)} copy(bf16[256,128]{1,0:T(8,128)(2,1)S(1)} %get-tuple-element.5) | data formatting | bytes 131072

commit v2 on v1

--- a/solution.py
+++ b/solution.py
@@ -104,6 +104,7 @@
     p_in,
     r_out,
     own_out,
+    f_in,
     r_in,
     load_sem,
     kv_send,
@@ -112,6 +113,7 @@
     p_recv,
     r_send,
     own_send,
+    f_recv,
     r_recv,
 ):
     me = lax.axis_index("seq")
@@ -165,15 +167,19 @@
         [remote(p_out.at[m, part], p_in.at[m, part], p_send.at[m, part], p_recv.at[m, part], partner) for part in range(2)]
         for m in range(3)
     ]
-    owners = [-2 - 4 * core, -6 + 4 * core, -4, -7 + 6 * core]
+    owners = {0: -2 - 4 * core, 1: -6 + 4 * core, 3: -7 + 6 * core}
+    first_slot = {0: 0, 1: 2, 3: 4}
 
     def to_owner(m, part):
-        slot = 2 * m + jnp.where(head == part, 0, 1)
+        slot = first_slot[m] + jnp.where(head == part, 0, 1)
         to = {"seq": seq(owners[m]), "head": part}
         return remote(r_out.at[m, part], r_in.at[slot], r_send.at[m, part], r_recv.at[slot], to)
 
-    returns = [[to_owner(m, part) for part in range(2)] for m in range(4)]
-    own_half = remote(own_out, r_in.at[8], own_send, r_recv.at[8], across)
+    returns = {m: [to_owner(m, part) for part in range(2)] for m in owners}
+    returns[2] = [
+        remote(r_out.at[2, part], f_in.at[part], r_send.at[2, part], f_recv.at[part], at(2 - 4 * core)) for part in range(2)
+    ]
+    own_half = remote(own_out, r_in.at[6], own_send, r_recv.at[6], across)
 
     for load in loads[:4]:
         load.wait()
@@ -208,6 +214,9 @@
         if m < 3:
             to_partner[m][part].wait_recv()
             total = total + p_in[m, part].astype(F32)
+        if m == 1:
+            returns[2][part].wait_recv()
+            total = total + f_in[part].astype(F32)
         r_out[m, part] = total.astype(BF16)
         returns[m][part].start()
 
@@ -269,12 +278,12 @@
             dq_ref[j * TILE : (j + 1) * TILE, h * DH : (h + 1) * DH] = tile
 
     total = accs[OWN, head]
-    for slot in (6, 7, 8, 0, 1, 4, 5, 2, 3):
+    for slot in (4, 5, 6, 0, 1, 2, 3):
         pltpu.make_async_copy(r_in.at[slot], r_in.at[slot], r_recv.at[slot]).wait()
         total = total + r_in[slot].astype(F32)
     dk_ref[...] = total[0].astype(BF16)
     dv_ref[...] = total[1].astype(BF16)
-    for copies in [send_e, send_l, send_c, pass_e, pass_on, pass_l, pass_f] + to_partner + returns + [[own_half]]:
+    for copies in [send_e, send_l, send_c, pass_e, pass_on, pass_l, pass_f] + to_partner + list(returns.values()) + [[own_half]]:
         for copy in copies:
             copy.wait_send()
 
@@ -315,7 +324,8 @@
                 pltpu.VMEM((3, 2) + half, BF16),
                 pltpu.VMEM((4, 2) + half, BF16),
                 pltpu.VMEM(half, BF16),
-                pltpu.VMEM((9,) + half, BF16),
+                pltpu.VMEM((2,) + half, BF16),
+                pltpu.VMEM((7,) + half, BF16),
                 dma((8,)),
                 dma((8, 2)),
                 dma((8, 2)),
@@ -323,7 +333,8 @@
                 dma((3, 2)),
                 dma((4, 2)),
                 dma,
-                dma((9,)),
+                dma((2,)),
+                dma((7,)),
             ],
             compiler_params=pltpu.CompilerParams(
                 collective_id=0, has_side_effects=True, vmem_limit_bytes=60 * 2**20

time: 48.9 us -> 47.7 us (0.975)
  Pallas kernels: 46.1 us -> 44.8 us
    pallas_call x1, Pallas kernels: 46.1 us -> 44.8 us  [shards(): pl.pallas_call(functools.partial(kernel, n), out_shape=(pltpu.VMEM(query....]
where the time goes in v2:
time: 47.7 us; the launch traced here: 47.5 us
  Pallas kernels  44.8 us (94%)
  local copies, waits for them, and re-layouts  2.05 us (4%)
  between operations  0.64 us (1%)
    pallas_call x1, Pallas kernels, shards(): pl.pallas_call(functools.partial(kernel, n), out_shape=(pltpu.VMEM(query....  44.8 us
    unnamed x3, local copies, waits for them, and re-layouts  2.05 us

profile of v2, /device:TPU:8, one launch (start us, length us, event | category | flops | bytes accessed | tf_op | source)
XLA Modules:
  0.0 47.5 jit_solution(8014068232690173400)
XLA Ops:
  0.6 44.8 %window_grads.1 = (bf16[512,512]{1,0:T(8,128)(2,1)S(1)}, bf16[256,128]{1,0:T(8,128)(2,1)S(1)}, bf16[256,128]{1,0:T(8,128)(2,1)S(1)}) custom-call(s32[128]{0:T(128)} %stripe.1, bf16[512,512]{1,0:T(8,128)(2,1)} %q_hbm.1, bf16[512,128]{1,0:T(8,128)(2,1)} %k_hbm.1, bf16[512,128]{1,0:T(8,128)(2,1)} %v_hbm.1, bf16[512,512]{1,0:T(8,128)(2,1)} %o_hbm.1, ...), custom_call_target="tpu_custom_call" | custom-call | tf_op jit(solution)/shard_map/window_grads/pallas_call | solution.py:299
  45.5 0.8 %copy.13 = bf16[512,512]{1,0:T(8,128)(2,1)} copy(bf16[512,512]{1,0:T(8,128)(2,1)S(1)} %get-tuple-element.3) | data formatting | bytes 1048576
  46.3 0.6 %copy.14 = bf16[256,128]{1,0:T(8,128)(2,1)} copy(bf16[256,128]{1,0:T(8,128)(2,1)S(1)} %get-tuple-element.4) | data formatting | bytes 131072
  46.9 0.6 %copy.15 = bf16[256,128]{1,0:T(8,128)(2,1)} copy(bf16[256,128]{1,0:T(8,128)(2,1)S(1)} %get-tuple-element.5) | data formatting | bytes 131072

commit v3 on v2

--- a/solution.py
+++ b/solution.py
@@ -84,8 +84,7 @@
     g_hbm,
     lse_hbm,
     dq_ref,
-    dk_ref,
-    dv_ref,
+    sums_ref,
     q_ref,
     o_ref,
     g_ref,
@@ -140,8 +139,10 @@
         load.start()
 
     barrier = pltpu.get_barrier_semaphore()
-    peers = [partner, across, at(2), at(-2), at(6), at(-6), at(4), at(-4), at(14 * core - 7)]
-    peers += [{"seq": peer["seq"], "head": 1 - head} for peer in [partner] + peers[2:]]
+    came_from = [at(-2 - 4 * core), at(-6 + 4 * core), at(-2 + 4 * core), at(-7 + 6 * core)]
+    read_by = [at(2 + 4 * core), at(6 - 4 * core), at(1 + 6 * core)]
+    peers = [partner, across] + came_from + read_by
+    peers += [{"seq": peer["seq"], "head": 1 - head} for peer in read_by]
     for peer in peers:
         pl.semaphore_signal(barrier, inc=1, device_id=peer, device_id_type=pl.DeviceIdType.MESH)
 
@@ -281,8 +282,7 @@
     for slot in (4, 5, 6, 0, 1, 2, 3):
         pltpu.make_async_copy(r_in.at[slot], r_in.at[slot], r_recv.at[slot]).wait()
         total = total + r_in[slot].astype(F32)
-    dk_ref[...] = total[0].astype(BF16)
-    dv_ref[...] = total[1].astype(BF16)
+    sums_ref[...] = total
     for copies in [send_e, send_l, send_c, pass_e, pass_on, pass_l, pass_f] + to_partner + list(returns.values()) + [[own_half]]:
         for copy in copies:
             copy.wait_send()
@@ -296,15 +296,14 @@
         anywhere = pl.BlockSpec(memory_space=pl.ANY)
         vmem = pl.BlockSpec(memory_space=pltpu.VMEM)
         dma = pltpu.SemaphoreType.DMA
-        return pl.pallas_call(
+        grad_query, sums = pl.pallas_call(
             functools.partial(kernel, n),
             out_shape=(
                 pltpu.VMEM(query.shape, BF16),
-                pltpu.VMEM((HALF, DH), BF16),
-                pltpu.VMEM((HALF, DH), BF16),
+                pltpu.VMEM(half, F32),
             ),
             in_specs=[pl.BlockSpec(memory_space=pltpu.SMEM)] + [anywhere] * 6,
-            out_specs=(vmem, vmem, vmem),
+            out_specs=(vmem, vmem),
             scratch_shapes=[
                 pltpu.VMEM((ROWS, HEADS * DH), BF16),
                 pltpu.VMEM((ROWS, HEADS * DH), BF16),
@@ -341,6 +340,7 @@
             ),
             name="window_grads",
         )(stripe, query, key_rows, value_rows, output, grad_output, log_norm)
+        return grad_query, sums[0].astype(BF16), sums[1].astype(BF16)
 
     placed = (
         P("seq", "head"),

time: 47.7 us -> 46.6 us (0.977)
  local copies, waits for them, and re-layouts: 2.05 us -> 1.45 us
  Pallas kernels: 44.8 us -> 44.2 us
    unnamed x3 -> x1, local copies, waits for them, and re-layouts: 2.05 us -> 0.79 us
    pallas_call x1, Pallas kernels: 44.8 us -> 44.2 us  [shards(): pl.pallas_call(functools.partial(kernel, n), out_shape=(pltpu.VMEM(query....]
    convert_element_type x0 -> x1, local copies, waits for them, and re-layouts: none -> 0.66 us  [shards(): return (grad_query, sums[0].astype(BF16), sums[1].astype(BF16))]
where the time goes in v3:
time: 46.6 us; the launch traced here: 46.3 us
  Pallas kernels  44.2 us (95%)
  local copies, waits for them, and re-layouts  1.45 us (3%)
  between operations  0.65 us (1%)
    pallas_call x1, Pallas kernels, shards(): pl.pallas_call(functools.partial(kernel, n), out_shape=(pltpu.VMEM(query....  44.2 us

profile of v3, /device:TPU:8, one launch (start us, length us, event | category | flops | bytes accessed | tf_op | source)
XLA Modules:
  0.0 46.3 jit_solution(5915280553930781734)
XLA Ops:
  0.6 44.2 %window_grads.1 = (bf16[512,512]{1,0:T(8,128)(2,1)S(1)}, f32[2,256,128]{2,1,0:T(8,128)S(1)}) custom-call(s32[128]{0:T(128)} %stripe.1, bf16[512,512]{1,0:T(8,128)(2,1)} %q_hbm.1, bf16[512,128]{1,0:T(8,128)(2,1)} %k_hbm.1, bf16[512,128]{1,0:T(8,128)(2,1)} %v_hbm.1, bf16[512,512]{1,0:T(8,128)(2,1)} %o_hbm.1, bf16[512,512]{1,0:T(8,128)(2,1)} %g_hbm.1, ...), custom_call_target="tpu_custom_call" | custom-call | tf_op jit(solution)/shard_map/window_grads/pallas_call | solution.py:299
  44.8 0.7 %slice_bitcast_fusion = (bf16[256,128]{1,0:T(8,128)(2,1)}, bf16[256,128]{1,0:T(8,128)(2,1)}) fusion(bf16[2,256,128]{2,1,0:T(8,128)(2,1)S(1)} %convert.4), kind=kLoop, calls=%fused_computation | loop fusion | bytes 262144 | tf_op jit(solution)/shard_map/convert_element_type | solution.py:343
  45.5 0.8 %copy.11 = bf16[512,512]{1,0:T(8,128)(2,1)} copy(bf16[512,512]{1,0:T(8,128)(2,1)S(1)} %get-tuple-element.9) | data formatting | bytes 1048576
  (1 shorter events, 0.0 us)

commit v4 on v3

--- a/solution.py
+++ b/solution.py
@@ -140,7 +140,7 @@
 
     barrier = pltpu.get_barrier_semaphore()
     came_from = [at(-2 - 4 * core), at(-6 + 4 * core), at(-2 + 4 * core), at(-7 + 6 * core)]
-    read_by = [at(2 + 4 * core), at(6 - 4 * core), at(1 + 6 * core)]
+    read_by = [at(6 - 4 * core), at(1 + 6 * core)]
     peers = [partner, across] + came_from + read_by
     peers += [{"seq": peer["seq"], "head": 1 - head} for peer in read_by]
     for peer in peers:
@@ -168,8 +168,8 @@
         [remote(p_out.at[m, part], p_in.at[m, part], p_send.at[m, part], p_recv.at[m, part], partner) for part in range(2)]
         for m in range(3)
     ]
-    owners = {0: -2 - 4 * core, 1: -6 + 4 * core, 3: -7 + 6 * core}
-    first_slot = {0: 0, 1: 2, 3: 4}
+    owners = {1: -6 + 4 * core, 3: -7 + 6 * core}
+    first_slot = {1: 0, 3: 2}
 
     def to_owner(m, part):
         slot = first_slot[m] + jnp.where(head == part, 0, 1)
@@ -177,10 +177,12 @@
         return remote(r_out.at[m, part], r_in.at[slot], r_send.at[m, part], r_recv.at[slot], to)
 
     returns = {m: [to_owner(m, part) for part in range(2)] for m in owners}
-    returns[2] = [
-        remote(r_out.at[2, part], f_in.at[part], r_send.at[2, part], f_recv.at[part], at(2 - 4 * core)) for part in range(2)
-    ]
-    own_half = remote(own_out, r_in.at[6], own_send, r_recv.at[6], across)
+    for m in (0, 2):
+        returns[m] = [
+            remote(r_out.at[m, part], f_in.at[m // 2, part], r_send.at[m, part], f_recv.at[m // 2, part], at(2 - 4 * core))
+            for part in range(2)
+        ]
+    own_half = remote(own_out, r_in.at[4], own_send, r_recv.at[4], across)
 
     for load in loads[:4]:
         load.wait()
@@ -215,9 +217,9 @@
         if m < 3:
             to_partner[m][part].wait_recv()
             total = total + p_in[m, part].astype(F32)
-        if m == 1:
-            returns[2][part].wait_recv()
-            total = total + f_in[part].astype(F32)
+        if m in (1, 2):
+            returns[2 if m == 1 else 0][part].wait_recv()
+            total = total + f_in[2 - m, part].astype(F32)
         r_out[m, part] = total.astype(BF16)
         returns[m][part].start()
 
@@ -279,7 +281,7 @@
             dq_ref[j * TILE : (j + 1) * TILE, h * DH : (h + 1) * DH] = tile
 
     total = accs[OWN, head]
-    for slot in (4, 5, 6, 0, 1, 2, 3):
+    for slot in (2, 3, 4, 0, 1):
         pltpu.make_async_copy(r_in.at[slot], r_in.at[slot], r_recv.at[slot]).wait()
         total = total + r_in[slot].astype(F32)
     sums_ref[...] = total
@@ -323,8 +325,8 @@
                 pltpu.VMEM((3, 2) + half, BF16),
                 pltpu.VMEM((4, 2) + half, BF16),
                 pltpu.VMEM(half, BF16),
-                pltpu.VMEM((2,) + half, BF16),
-                pltpu.VMEM((7,) + half, BF16),
+                pltpu.VMEM((2, 2) + half, BF16),
+                pltpu.VMEM((5,) + half, BF16),
                 dma((8,)),
                 dma((8, 2)),
                 dma((8, 2)),
@@ -332,8 +334,8 @@
                 dma((3, 2)),
                 dma((4, 2)),
                 dma,
-                dma((2,)),
-                dma((7,)),
+                dma((2, 2)),
+                dma((5,)),
             ],
             compiler_params=pltpu.CompilerParams(
                 collective_id=0, has_side_effects=True, vmem_limit_bytes=60 * 2**20

time: 46.6 us -> 45.7 us (0.981)
  Pallas kernels: 44.2 us -> 43.3 us
    pallas_call x1, Pallas kernels: 44.2 us -> 43.3 us  [shards(): pl.pallas_call(functools.partial(kernel, n), out_shape=(pltpu.VMEM(query....]
where the time goes in v4:
time: 45.7 us; the launch traced here: 45.4 us
  Pallas kernels  43.3 us (95%)
  local copies, waits for them, and re-layouts  1.45 us (3%)
  between operations  0.65 us (1%)
    pallas_call x1, Pallas kernels, shards(): pl.pallas_call(functools.partial(kernel, n), out_shape=(pltpu.VMEM(query....  43.3 us

profile of v4, /device:TPU:8, one launch (start us, length us, event | category | flops | bytes accessed | tf_op | source)
XLA Modules:
  0.0 45.4 jit_solution(5502803933506267237)
XLA Ops:
  0.6 43.3 %window_grads.1 = (bf16[512,512]{1,0:T(8,128)(2,1)S(1)}, f32[2,256,128]{2,1,0:T(8,128)S(1)}) custom-call(s32[128]{0:T(128)} %stripe.1, bf16[512,512]{1,0:T(8,128)(2,1)} %q_hbm.1, bf16[512,128]{1,0:T(8,128)(2,1)} %k_hbm.1, bf16[512,128]{1,0:T(8,128)(2,1)} %v_hbm.1, bf16[512,512]{1,0:T(8,128)(2,1)} %o_hbm.1, bf16[512,512]{1,0:T(8,128)(2,1)} %g_hbm.1, ...), custom_call_target="tpu_custom_call" | custom-call | tf_op jit(solution)/shard_map/window_grads/pallas_call | solution.py:301
  44.0 0.7 %slice_bitcast_fusion = (bf16[256,128]{1,0:T(8,128)(2,1)}, bf16[256,128]{1,0:T(8,128)(2,1)}) fusion(bf16[2,256,128]{2,1,0:T(8,128)(2,1)S(1)} %convert.4), kind=kLoop, calls=%fused_computation | loop fusion | bytes 262144 | tf_op jit(solution)/shard_map/convert_element_type | solution.py:345
  44.6 0.8 %copy.11 = bf16[512,512]{1,0:T(8,128)(2,1)} copy(bf16[512,512]{1,0:T(8,128)(2,1)S(1)} %get-tuple-element.9) | data formatting | bytes 1048576
  (1 shorter events, 0.0 us)

commit v5 on v4

--- a/solution.py
+++ b/solution.py
@@ -229,17 +229,13 @@
             own_out[...] = accs[OWN, part].astype(BF16)
             own_half.start()
 
-        if part == 1:
-
-            @pl.when(s == OWN)
-            def _():
-                for copy in send_c:
-                    copy.start()
-
-            @pl.when(s == E)
-            def _():
-                for copy in send_l:
-                    copy.start()
+        for when, copies in ((0, send_c), (1, send_l)):
+            if part == when:
+
+                @pl.when(s == E)
+                def _():
+                    for copy in copies:
+                        copy.start()
 
         for m, block in enumerate((PE, PL, PF)):
 

time: 45.7 us -> 47 us (1.028)
  the two profiles are of different devices: /device:TPU:8 before, /device:TPU:18 now
where the time goes in v5:
time: 47 us; the launch traced here: 46.8 us
  Pallas kernels  44.7 us (95%)
  local copies, waits for them, and re-layouts  1.45 us (3%)
  between operations  0.65 us (1%)
    pallas_call x1, Pallas kernels, shards(): pl.pallas_call(functools.partial(kernel, n), out_shape=(pltpu.VMEM(query....  44.7 us

profile of v5, /device:TPU:18, one launch (start us, length us, event | category | flops | bytes accessed | tf_op | source)
XLA Modules:
  0.0 46.8 jit_solution(12903207554130722452)
XLA Ops:
  0.6 44.7 %window_grads.1 = (bf16[512,512]{1,0:T(8,128)(2,1)S(1)}, f32[2,256,128]{2,1,0:T(8,128)S(1)}) custom-call(s32[128]{0:T(128)} %stripe.1, bf16[512,512]{1,0:T(8,128)(2,1)} %q_hbm.1, bf16[512,128]{1,0:T(8,128)(2,1)} %k_hbm.1, bf16[512,128]{1,0:T(8,128)(2,1)} %v_hbm.1, bf16[512,512]{1,0:T(8,128)(2,1)} %o_hbm.1, bf16[512,512]{1,0:T(8,128)(2,1)} %g_hbm.1, ...), custom_call_target="tpu_custom_call" | custom-call | tf_op jit(solution)/shard_map/window_grads/pallas_call | solution.py:297
  45.4 0.7 %slice_bitcast_fusion = (bf16[256,128]{1,0:T(8,128)(2,1)}, bf16[256,128]{1,0:T(8,128)(2,1)}) fusion(bf16[2,256,128]{2,1,0:T(8,128)(2,1)S(1)} %convert.4), kind=kLoop, calls=%fused_computation | loop fusion | bytes 262144 | tf_op jit(solution)/shard_map/convert_element_type | solution.py:341
  46.1 0.8 %copy.11 = bf16[512,512]{1,0:T(8,128)(2,1)} copy(bf16[512,512]{1,0:T(8,128)(2,1)S(1)} %get-tuple-element.9) | data formatting | bytes 1048576
  (1 shorter events, 0.0 us)
